TPU v7x, 32 devices: a whole 2x2x4 slice. The times are simulated.
32 devices in a mesh: dp: 4 (over z), stage: 2 (over y), tp: 4 (over x, core).
Axes of the slice: x: 2, y: 2, z: 4, core: 2. Of those that a mesh axis runs over, the one named last changes fastest.
Arguments:
- act_in: bfloat16 [2, 32, 14, 14, 1024], P('stage', ('dp', 'tp'))
- w_conv: bfloat16 [2, 3, 3, 1024, 1024], P('stage', None, None, None, 'tp')
- gamma_vec: float32 [2, 1024], P('stage', 'tp')
- beta_vec: float32 [2, 1024], P('stage', 'tp')
- z_grad: bfloat16 [2, 32, 14, 14, 1024], P('stage', 'dp', None, None, 'tp')
Outputs:
- output 1: bfloat16 [2, 32, 14, 14, 1024], P('stage', 'dp', None, None, 'tp')
- output 2: bfloat16 [2, 32, 14, 14, 1024], P('stage', ('dp', 'tp'))
- output 3: float32 [2, 3, 3, 1024, 1024], P('stage', None, None, None, 'tp')
All inputs are finite; a program needn't handle non-finite values.
Results may differ from a plain program's by a relative error of at most 0.00473.
Values are sent between devices in bfloat16 or wider.
A program may use at most 1 GiB of HBM per device.

v0:
```python
import jax
import jax.numpy as jnp
from jax import lax
from jax.sharding import PartitionSpec as P


def conv_fwd(images, kernel):
    return lax.conv_general_dilated(images, kernel, (1, 1), 'SAME', dimension_numbers=('NHWC', 'HWIO', 'NHWC'), preferred_element_type=jnp.float32)


def conv_input_grad(grad_map, kernel):
    flipped = lax.rev(kernel, (0, 1))
    return lax.conv_general_dilated(grad_map, flipped, (1, 1), 'SAME', dimension_numbers=('NHWC', 'HWOI', 'NHWC'), preferred_element_type=jnp.float32)


def conv_kernel_grad(images, grad_map):
    return lax.conv_general_dilated(images, grad_map, (1, 1), ((1, 1), (1, 1)), dimension_numbers=('CHWN', 'IHWO', 'HWNC'), preferred_element_type=jnp.float32)


def solution(mesh):
    act_spec = P('stage', ('dp', 'tp'))
    w_spec = P('stage', None, None, None, 'tp')
    vec_spec = P('stage', 'tp')
    chan_spec = P('stage', 'dp', None, None, 'tp')

    def device_step(act_in, w_conv, gamma_vec, beta_vec, z_grad):
        on_conv = lax.axis_index('stage') == 1
        arrived = lax.ppermute(act_in[0], 'stage', perm=[(0, 1)])
        group_act = lax.all_gather(arrived, 'tp', axis=0, tiled=True)
        kernel = w_conv[0]
        gamma_row = gamma_vec[0]
        beta_row = beta_vec[0]
        pre_act = conv_fwd(group_act, kernel)
        affine = pre_act * gamma_row + beta_row
        z_local = jnp.maximum(affine, 0.0).astype(jnp.bfloat16)
        grad_pre = jnp.where(affine > 0, z_grad[0] * gamma_row, 0.0).astype(jnp.bfloat16)
        act_part = conv_input_grad(grad_pre, kernel)
        act_mine = lax.psum_scatter(act_part, 'tp', scatter_dimension=0, tiled=True).astype(jnp.bfloat16)
        act_back = lax.ppermute(act_mine, 'stage', perm=[(1, 0)])
        w_part = conv_kernel_grad(group_act, grad_pre)
        w_total = lax.psum(w_part, 'dp')
        z_keep = jnp.where(on_conv, z_local, jnp.zeros_like(z_local))
        w_keep = jnp.where(on_conv, w_total, jnp.zeros_like(w_total))
        return z_keep[None], act_back[None], w_keep[None]

    return jax.shard_map(device_step, mesh=mesh, in_specs=(act_spec, w_spec, vec_spec, vec_spec, chan_spec), out_specs=(chan_spec, act_spec, w_spec), check_vma=False)
```

profile of v0, /device:TPU:6, one launch (start us, length us, event | category | flops | bytes accessed | tf_op | source)
XLA Modules:
  0.0 429.9 jit_solution(2327424803040459818)
XLA Ops:
  7.2 0.0 copy-start.2
  7.2 0.0 copy-start.3
  7.2 0.0 all-gather.2.cloned.1.call-start
  7.2 1.3 collective-permute-start
  8.5 20.2 %collective-permute-done = bf16[2,14,14,1024]{3,0,2,1:T(2,128)(2,1)S(1)} collective-permute-done((bf16[2,14,14,1024]{3,0,2,1:T(2,128)(2,1)}, bf16[2,14,14,1024]{3,0,2,1:T(2,128)(2,1)S(1)}, u32[]{:S(2)}, u32[]{:S(2)}) %collective-permute-start) | collective-permute-done | bytes 802848 | tf_op jit(solution)/shard_map/ppermute | solution.py:28
  28.8 1.1 copy.11
  29.9 0.0 all-gather.2.cloned.1.call-update
  29.9 0.0 all-reduce.4.cloned.1.call-start
  30.0 31.6 %all-gather.2.cloned.1.call-done = bf16[8,14,14,1024]{3,2,1,0:T(8,128)(2,1)} async-done(((bf16[2,14,14,1024]{3,2,1,0:T(8,128)(2,1)}), bf16[8,14,14,1024]{3,2,1,0:T(8,128)(2,1)}) %all-gather.2.cloned.1.call-update) | async-done | bytes 3211280 | tf_op jit(solution)/shard_map/all_gather | solution.py:29
  61.6 0.0 copy-done.2
  61.6 0.0 copy-done.3
  61.6 0.0 copy-start
  61.6 0.0 copy-start.1
  61.6 13.5 %fusion.21 = (u16[8,14,256]{2,0,1:T(8,128)(2,1)S(1)}, bf16[8,14,14,256]{3,0,2,1:T(8,128)(2,1)}) fusion(f32[256]{0:T(256)S(1)} %bitcast.27, f32[256]{0:T(256)S(1)} %bitcast.28, bf16[1,3,3,1024,256]{4,3,2,1,0:T(8,128)(2,1)} %param.6, bf16[8,14,14,1024]{3,2,1,0:T(8,128)(2,1)} %all-gather.2.cloned.1.call-done), kind=kOutput, calls=%fused_computation.19 | convolution fusion | flops 6714068992 | bytes 8792064 | tf_op jit(solution)/shard_map/conv_general_dilated | solution.py:8
  75.1 0.0 copy-done
  75.1 0.0 copy-done.1
  75.1 15.3 %fusion.4 = f32[3,3,1024,256]{3,2,1,0:T(8,128)} fusion(bf16[8,14,14,1024]{3,2,1,0:T(8,128)(2,1)S(1)} %copy-done, bf16[1,8,14,14,256]{4,1,3,2,0:T(8,128)(2,1)S(1)} %copy-done.1, f32[256]{0:T(256)S(1)} %bitcast.29, u16[8,14,256]{2,0,1:T(8,128)(2,1)S(1)} %get-tuple-element.3), kind=kOutput, calls=%fused_computation.5 | convolution fusion | flops 6714097664 | bytes 13509632 | tf_op jit(solution)/shard_map/conv_general_dilated | solution.py:17
  90.4 0.0 copy-start.4
  90.4 0.0 all-reduce.4.cloned.1.call-update
  90.4 0.6 copy-done.4
  91.0 0.6 dynamic-slice
  92.3 11.5 %fusion = f32[8,14,14,1024]{3,0,2,1:T(8,128)} fusion(bf16[1,3,3,1024,256]{4,3,2,1,0:T(8,128)(2,1)} %param.6, bf16[1,8,14,14,256]{4,1,3,2,0:T(8,128)(2,1)S(1)} %copy-done.1, f32[256]{0:T(256)S(1)} %bitcast.30, u16[8,14,256]{2,0,1:T(8,128)(2,1)S(1)} %get-tuple-element.3), kind=kOutput, calls=%fused_computation.1 | convolution fusion | flops 6714097664 | bytes 12002304 | tf_op jit(solution)/shard_map/conv_general_dilated | solution.py:13
  103.7 115.0 %all-reduce.5 = bf16[8,14,14,1024]{3,0,2,1:T(8,128)(2,1)S(1)} all-reduce(f32[8,14,14,1024]{3,0,2,1:T(8,128)} %fusion), channel_id=2, replica_groups=mesh['dp'=4,'stage'=2,'tp'=4] {'tp'}, use_global_device_ids=true, to_apply=%region_0.1.clone | all-reduce | flops 1605632 | bytes 9633792
  218.7 1.7 dynamic-slice_convert_fusion
  220.4 2.5 collective-permute-start.1
  222.9 2.2 fusion.20
  225.2 15.3 %collective-permute-done.1 = bf16[2,14,14,1024]{3,0,2,1:T(2,128)(2,1)S(1)} collective-permute-done((bf16[2,14,14,1024]{3,0,2,1:T(2,128)(2,1)}, bf16[2,14,14,1024]{3,0,2,1:T(2,128)(2,1)S(1)}, u32[]{:S(2)}, u32[]{:S(2)}) %collective-permute-start.1) | collective-permute-done | bytes 802848 | tf_op jit(solution)/shard_map/ppermute | solution.py:39
  240.4 173.6 %all-reduce.4.cloned.1.call-done = f32[3,3,1024,256]{3,2,1,0:T(8,128)} async-done(((f32[3,3,1024,256]{3,2,1,0:T(8,128)}), f32[3,3,1024,256]{3,2,1,0:T(8,128)}) %all-reduce.4.cloned.1.call-update) | async-done | bytes 9437200 | tf_op jit(solution)/shard_map/psum | solution.py:41
  414.1 8.1 %select_bitcast_fusion = f32[1,3,3,1024,256]{4,3,2,1,0:T(8,128)} fusion(f32[3,3,1024,256]{3,2,1,0:T(8,128)} %all-reduce.4.cloned.1.call-done, pred[]{:T(512)S(6)} %eq.3), kind=kLoop, calls=%fused_computation | loop fusion | flops 2359296 | bytes 18874368 | tf_op jit(solution)/shard_map/broadcast_in_dim | solution.py:44
  422.1 0.9 copy.30
Async XLA Ops:
  7.2 54.4 %copy-start.2 = (f32[1,256]{1,0:T(1,128)S(1)}, f32[1,256]{1,0:T(1,128)}, u32[]{:S(2)}) copy-start(f32[1,256]{1,0:T(1,128)} %param.8) | copy-start | bytes 3076
  7.2 54.4 %copy-start.3 = (f32[1,256]{1,0:T(1,128)S(1)}, f32[1,256]{1,0:T(1,128)}, u32[]{:S(2)}) copy-start(f32[1,256]{1,0:T(1,128)} %param.7) | copy-start | bytes 3076
  7.2 54.4 %all-gather.2.cloned.1.call-start = ((), (), s32[]{:S(2)}) async-start(), calls=%async_computation | async-start | bytes 4587520 | tf_op jit(solution)/shard_map/all_gather | solution.py:29
  7.2 21.5 %collective-permute-start = (bf16[2,14,14,1024]{3,0,2,1:T(2,128)(2,1)}, bf16[2,14,14,1024]{3,0,2,1:T(2,128)(2,1)S(1)}, u32[]{:S(2)}, u32[]{:S(2)}) collective-permute-start(bf16[2,14,14,1024]{3,0,2,1:T(2,128)(2,1)} %bitcast.26), channel_id=1, source_target_pairs={{0,4},{1,5},{2,6},{3,7},{8,12},{9,13},{10,14},{11,15},{16,20},{17,... | collective-permute-start | bytes 2408456 | tf_op jit(solution)/shard_map/ppermute | solution.py:28
  29.9 384.1 %all-reduce.4.cloned.1.call-start = ((), (), s32[]{:S(2)}) async-start(), calls=%async_computation.1 | async-start | bytes 18874368 | tf_op jit(solution)/shard_map/psum | solution.py:41
  61.6 13.5 %copy-start = (bf16[8,14,14,1024]{3,2,1,0:T(8,128)(2,1)S(1)}, bf16[8,14,14,1024]{3,2,1,0:T(8,128)(2,1)}, u32[]{:S(2)}) copy-start(bf16[8,14,14,1024]{3,2,1,0:T(8,128)(2,1)} %all-gather.2.cloned.1.call-done) | copy-start | bytes 9633796
  61.6 13.5 %copy-start.1 = (bf16[1,8,14,14,256]{4,1,3,2,0:T(8,128)(2,1)S(1)}, bf16[1,8,14,14,256]{4,1,3,2,0:T(8,128)(2,1)}, u32[]{:S(2)}) copy-start(bf16[1,8,14,14,256]{4,1,3,2,0:T(8,128)(2,1)} %param.9) | copy-start | bytes 2408452
  90.4 0.7 copy-start.4
  220.4 20.0 %collective-permute-start.1 = (bf16[2,14,14,1024]{3,0,2,1:T(2,128)(2,1)}, bf16[2,14,14,1024]{3,0,2,1:T(2,128)(2,1)S(1)}, u32[]{:S(2)}, u32[]{:S(2)}) collective-permute-start(bf16[2,14,14,1024]{3,0,2,1:T(2,128)(2,1)} %dynamic-slice_convert_fusion), channel_id=1, source_target_pairs={{4,0},{5,1},{6,2},{7,3},{12,8},{13,9},{14,10},{15,11},{20,16},{21,... | collective-permute-start | bytes 2408456 | tf_op jit(solution)/shard_map/ppermute | solution.py:39
Sparse Core Ops, SparseCore 0:
  30.1 31.5 all-gather.1
  90.5 323.4 all-reduce.3
where the time goes:
time: 430 us
  waiting for transfers between devices  241 us (56%)
  blocking collectives  115 us (27%)
  matrix products  40.2 us (9%)
  between operations  14.8 us (3%)
  other arithmetic  10.3 us (2%)
  local copies, waits for them, and re-layouts  5 us (1%)
    psum x1, waiting for transfers between devices, device_step(): w_total = lax.psum(w_part, 'dp')  174 us
    unnamed x1, blocking collectives  115 us
    all_gather x1, waiting for transfers between devices, device_step(): group_act = lax.all_gather(arrived, 'tp', axis=0, tiled=True)  31.6 us
    ppermute x1, waiting for transfers between devices, device_step(): arrived = lax.ppermute(act_in[0], 'stage', perm=[(0, 1)])  20.2 us
    ppermute x1, waiting for transfers between devices, device_step(): act_back = lax.ppermute(act_mine, 'stage', perm=[(1, 0)])  15.3 us
    conv_general_dilated x1, matrix products, conv_kernel_grad(): lax.conv_general_dilated(images, grad_map, (1, 1), ((1, 1), (1, 1)), dime...  15.3 us
    conv_general_dilated x1, matrix products, conv_fwd(): lax.conv_general_dilated(images, kernel, (1, 1), 'SAME', dimension_number...  13.5 us
    conv_general_dilated x1, matrix products, conv_input_grad(): lax.conv_general_dilated(grad_map, flipped, (1, 1), 'SAME', dimension_num...  11.5 us
  transfers between devices with their start and end apart: 4, of which 4 were waited for; matrix products, arithmetic and copies ran while one was open for 4% of the time, Pallas kernels for 0%

commit v1 on v0

v1 whole, which is shorter than its diff:
```python
import functools

import jax
import jax.numpy as jnp
from jax import lax
from jax.experimental import pallas as pl
from jax.experimental.pallas import tpu as pltpu
from jax.sharding import PartitionSpec as P

MESH = pl.DeviceIdType.MESH
F32 = jnp.float32
BF16 = jnp.bfloat16

SIDE = 14
LINE = 16
ROWS = SIDE * LINE
IMG = 256
PAIR = 2 * IMG
NDP = 4
GROUPS = ((0, 1), (2, 3), (4, 5), (6, 7), (8, 9), (12, 13), (10, 14), (11, 15))


def widen(dst, n, src, m):
    dst[n] = jnp.zeros(dst.shape[1:], BF16)
    for h in range(SIDE):
        dst[n, pl.ds(h * LINE, SIDE), :] = src[m, h]


def body(x_ref, w_hbm, gamma_ref, beta_ref, dz_ref, z_ref, dx_ref, dw_ref,
         xbuf, wbuf, gbuf, gs, xt, dxp, dxd, dxx, xs, dxin, dzp,
         w_sem, x_recv, y_send, yf_send, ring_send, x0_send, hop_send, near_send, far_send, early_send,
         g_recv, g_send, d_recv, d_send, h_recv, h_send, b_recv, b_send, m_recv, m_send):
    dp = lax.axis_index('dp')
    stage = lax.axis_index('stage')
    tp = lax.axis_index('tp')
    col, core = tp // 2, tp % 2
    up = (dp + 1) % NDP
    down = (dp + NDP - 1) % NDP
    twin = col * 2 + (1 - core)
    across = (1 - col) * 2 + core
    ci = x_ref.shape[-1]
    co = dz_ref.shape[-1]

    w_copy = pltpu.make_async_copy(w_hbm, wbuf, w_sem)

    @pl.when(stage == 1)
    def _():
        w_copy.start()

    @pl.when(stage == 0)
    def _():
        for i in range(2):
            widen(xs, i, x_ref, i)

    barrier = pltpu.get_barrier_semaphore()
    for peer in ((dp, 1 - stage, tp), (up, stage, tp), (down, stage, tp), (dp, stage, twin), (dp, stage, across)):
        pl.semaphore_signal(barrier, inc=1, device_id=peer, device_id_type=MESH)
    pl.semaphore_wait(barrier, 5)

    def pair(k, j, i):
        return (k * 2 + j) * 2 + i

    def xrows(k, rel, i):
        return xbuf.at[pl.ds(LINE + (pair(k, rel // 2, i) * 2 + rel % 2) * IMG, ROWS), :]

    def copy(src, dst, send, recv, peer):
        return pltpu.make_async_remote_copy(src_ref=src, dst_ref=dst, send_sem=send, recv_sem=recv, device_id=peer, device_id_type=MESH)

    home = (dp, 0, tp)
    conv = (dp, 1, tp)

    def x_source(k, i):
        return xs.at[i] if k == 0 else xrows(k, 0, i)

    def y_copy(k, i):
        return copy(x_source(k, i), xrows(k, 0, i), y_send.at[k, i], x_recv.at[k, 0, i], conv)

    def ring_copy(k, i):
        return copy(x_source(k - 1, i), xrows(k, 0, i), ring_send.at[k, i], x_recv.at[k, 0, i], (up, 0, tp))

    def x0_copy(i):
        return copy(xrows(2, 0, i), xrows(2, 2, i), x0_send.at[i], x_recv.at[2, 2, i], (dp, 0, across))

    def yf_copy(i):
        return copy(xrows(2, 2, i), xrows(2, 2, i), yf_send.at[i], x_recv.at[2, 2, i], conv)

    def hop_copy(k, i):
        return copy(xrows(k, 0, i), xrows(k, 2, i), hop_send.at[k, i], x_recv.at[k, 2, i], (dp, 1, across))

    def early_copy():
        return copy(xrows(0, 0, 0), xrows(1, 0, 0), early_send, x_recv.at[1, 0, 0], (up, 1, tp))

    def near_copy(k, i):
        return copy(xrows(k, 0, i), xrows(k, 1, i), near_send.at[k, i], x_recv.at[k, 1, i], (dp, 1, twin))

    def far_copy(k, i):
        return copy(xrows(k, 2, i), xrows(k, 3, i), far_send.at[k, i], x_recv.at[k, 3, i], (dp, 1, twin))

    def g_copy(k, p):
        rows = pl.ds(0, ROWS)
        return copy(gbuf.at[(k - 1) * 4 + p, :, rows, :], gbuf.at[k * 4 + p, :, rows, :], g_send.at[k, p], g_recv.at[k, p], (up, 1, tp))

    def d_copy(p):
        return copy(dxp.at[p, 1, pl.ds(0, ROWS), :], dxd.at[p], d_send.at[p], d_recv.at[p], (dp, 1, twin))

    own = pl.ds(0, ROWS)

    def h_copy():
        return copy(dxp.at[2, 0, own, :], dxx, h_send, h_recv, (dp, 1, across))

    def b_copy():
        return copy(xs.at[0], dxin, b_send, b_recv, home)

    def m_far():
        return copy(dxp.at[3, 0, own, :], dxd.at[0], m_send.at[0], m_recv.at[0], home)

    def m_cross():
        return copy(dxd.at[0], dxd.at[1], m_send.at[1], m_recv.at[1], (dp, 0, across))

    def m_near():
        return copy(dxp.at[1, 0, own, :], dxd.at[2], m_send.at[2], m_recv.at[2], home)

    def narrow(value):
        return value.reshape(SIDE, LINE, value.shape[-1])[:, :SIDE, :]

    @pl.when(stage == 0)
    def _():
        for i in range(2):
            y_copy(0, i).start()
            ring_copy(1, i).start()
        dw_ref[...] = jnp.zeros_like(dw_ref)
        z_ref[...] = jnp.zeros_like(z_ref)
        ring_copy(1, 0).wait_recv()
        ring_copy(2, 0).start()
        ring_copy(1, 1).wait_recv()
        y_copy(1, 1).start()
        ring_copy(2, 1).start()
        for i in range(2):
            ring_copy(2, i).wait_recv()
            y_copy(2, i).start()
            ring_copy(3, i).start()
            x0_copy(i).start()
        for i in range(2):
            ring_copy(3, i).wait_recv()
            y_copy(3, i).start()
        for i in range(2):
            x0_copy(i).wait_recv()
            yf_copy(i).start()
        m_far().wait_recv()
        m_cross().start()
        m_cross().wait_recv()
        m_near().wait_recv()
        dx_ref[1] = narrow((dxd[2] + dxd[1]).astype(BF16))
        b_copy().wait_recv()
        dx_ref[0] = narrow(dxin[...])
        for i in range(2):
            for k in range(4):
                if (k, i) != (1, 0):
                    y_copy(k, i).wait_send()
                if k:
                    ring_copy(k, i).wait_send()
            x0_copy(i).wait_send()
            yf_copy(i).wait_send()
        m_cross().wait_send()

    def near(k, i):
        y_copy(k, i).wait_recv()
        if k != 2:
            hop_copy(k, i).start()
        near_copy(k, i).start()

    def far(k, i):
        hop_copy(k, i).wait_recv()
        far_copy(k, i).start()

    def g_pass(k, p):
        g_copy(k, p).wait_recv()
        if k < 3:
            g_copy(k + 1, p).start()

    def rolled(value, shift):
        return pltpu.roll(value, shift % value.shape[0], axis=0)

    def forward(p):
        base = LINE + p * PAIR
        rows = PAIR - LINE
        total = None
        for dw in (0, 1, -1):
            part = None
            for dh in (-1, 0, 1):
                lhs = xbuf[pl.ds(pl.multiple_of(base + LINE * dh, LINE), rows), :]
                prod = jnp.dot(lhs, wbuf[(dh + 1) * 3 + dw + 1], preferred_element_type=F32)
                part = prod if part is None else part + prod
            part = rolled(part, -dw) if dw else part
            total = part if total is None else total + part
        affine = total * gamma_ref[...] + beta_ref[...]
        j, i = p // 2, p % 2
        for b in range(2):
            image = ((col + j - 2 * col * j) * 2 + (core + b - 2 * core * b)) * 2 + i
            part = affine[b * IMG:b * IMG + ROWS]
            z_ref[image] = narrow(jnp.maximum(part, 0.0).astype(BF16))
            dz = dzp[image].astype(F32)
            gbuf[p, b, pl.ds(0, ROWS), :] = jnp.where(part > 0, dz * gamma_ref[...], 0.0).astype(BF16)
        g_copy(1, p).start()

    def spread_g(p, at):
        g = gbuf[p].reshape(PAIR, co)
        gf = g.astype(F32)
        to = pl.ds(at, PAIR)
        gs[1, to, :] = g
        gs[2, to, :] = rolled(gf, 1).astype(BF16)
        gs[0, to, :] = rolled(gf, -1).astype(BF16)

    def input_grad(p):
        spread_g(p, LINE)

        def step(n, _):
            at = pl.ds(pl.multiple_of(n * 256, 256), 256)
            acc = None
            for dw in range(3):
                for dh in range(3):
                    lhs = gs[dw, pl.ds(LINE - LINE * (dh - 1), PAIR), :]
                    prod = lax.dot_general(lhs, wbuf[dh * 3 + dw, at, :], (((1,), (1,)), ((), ())), preferred_element_type=F32)
                    acc = prod if acc is None else acc + prod
            dxp[p, 0, :, at] = acc[:IMG]
            dxp[p, 1, :, at] = acc[IMG:]
            return 0

        lax.fori_loop(0, ci // 256, step, 0)
        d_copy(p).start()

    def dx_sum(p):
        d_copy(p).wait_recv()
        dxp[p, 0, own, :] += dxd[p]

    def kernel_grad(first, second):
        spread_g(first, LINE)
        spread_g(second, LINE + PAIR)

        def turn(q, _):
            row = jnp.where(q < 2, first * 2 + q, second * 2 + q - 2)
            at = pl.ds(pl.multiple_of(LINE + row * IMG, LINE), IMG)
            to = pl.ds(pl.multiple_of(q * IMG, IMG), IMG)
            for c in range(ci // 256):
                xt[pl.ds(c * 256, 256), to] = xbuf[at, pl.ds(c * 256, 256)].T
            return 0

        lax.fori_loop(0, 4, turn, 0)

        def step(dw, _):
            for dh in range(3):
                rhs = gs[dw, pl.ds(LINE - LINE * (dh - 1), 2 * PAIR), :]
                dw_ref[dh * 3 + dw] += jnp.dot(xt[...], rhs, preferred_element_type=F32)
            return 0

        lax.fori_loop(0, 3, step, 0)

    @pl.when(stage == 1)
    def _():
        xbuf[pl.ds(0, LINE), :] = jnp.zeros((LINE, ci), BF16)

        def clear(n, _):
            xbuf[pl.ds(pl.multiple_of(LINE + n * IMG + ROWS, LINE), IMG - ROWS), :] = jnp.zeros((IMG - ROWS, ci), BF16)
            return 0

        lax.fori_loop(0, 32, clear, 0)

        def clear_g(n, _):
            gbuf[n, :, pl.ds(ROWS, IMG - ROWS), :] = jnp.zeros((2, IMG - ROWS, co), BF16)
            return 0

        lax.fori_loop(0, 16, clear_g, 0)
        for dw in range(3):
            for at in (0, LINE + PAIR, LINE + 2 * PAIR):
                gs[dw, pl.ds(at, LINE), :] = jnp.zeros((LINE, co), BF16)

        def widen_dz(n, _):
            widen(dzp, n, dz_ref, n)
            return 0

        lax.fori_loop(0, 8, widen_dz, 0)
        dw_ref[...] = jnp.zeros_like(dw_ref)
        dx_ref[...] = jnp.zeros_like(dx_ref)
        w_copy.wait()

        near(0, 0)
        early_copy().start()
        near_copy(0, 0).wait_recv()
        forward(0)
        input_grad(0)
        near(0, 1)
        near(1, 0)
        far(0, 0)
        near_copy(0, 1).wait_recv()
        forward(1)
        g_pass(1, 0)
        far_copy(0, 0).wait_recv()
        forward(2)
        input_grad(2)
        far(0, 1)
        near(1, 1)
        far_copy(0, 1).wait_recv()
        forward(3)
        dx_sum(2)
        g_pass(1, 1)
        h_copy().start()
        input_grad(3)
        g_pass(1, 2)
        near(2, 0)
        dx_sum(3)
        far(1, 0)
        m_far().start()
        input_grad(1)
        dx_sum(0)
        g_pass(1, 3)
        g_pass(2, 0)
        dx_sum(1)
        g_pass(2, 1)
        m_near().start()

        def events(step):
            if step == 1:
                near(2, 1)
                far(1, 1)
                g_pass(2, 2)
                g_pass(2, 3)
            if step == 2:
                for i in range(2):
                    near_copy(1, i).wait_recv()
                g_pass(3, 0)
            if step == 3:
                near(3, 0)
                for i in range(2):
                    far_copy(1, i).wait_recv()
                g_pass(3, 1)
            if step == 4:
                near(3, 1)
                for i in range(2):
                    near_copy(2, i).wait_recv()
                g_pass(3, 2)
            if step == 5:
                for i in range(2):
                    near_copy(3, i).wait_recv()
                g_pass(3, 3)
                h_copy().wait_recv()
                xs[0] = (dxp[0, 0, own, :] + dxx[...]).astype(BF16)
                b_copy().start()
            if step >= 6:
                i = step - 6
                far(2, i)
                far(3, i)
                far_copy(2, i).wait_recv()
                far_copy(3, i).wait_recv()

        def run(step, _):
            for s in range(1, 8):
                @pl.when(step == s)
                def _(s=s):
                    events(s)

            first, second = (jnp.int32(v) for v in GROUPS[0])
            for s in range(1, 8):
                first = jnp.where(step == s, GROUPS[s][0], first)
                second = jnp.where(step == s, GROUPS[s][1], second)
            kernel_grad(first, second)
            return 0

        lax.fori_loop(0, 8, run, 0)

        for i in range(2):
            for k in range(4):
                near_copy(k, i).wait_send()
                far_copy(k, i).wait_send()
                if k != 2:
                    hop_copy(k, i).wait_send()
        early_copy().wait_send()
        for p in range(4):
            d_copy(p).wait_send()
            for k in range(1, 4):
                g_copy(k, p).wait_send()
        h_copy().wait_send()
        b_copy().wait_send()
        m_far().wait_send()
        m_near().wait_send()


def solution(mesh):
    act_spec = P('stage', ('dp', 'tp'))
    w_spec = P('stage', None, None, None, 'tp')
    vec_spec = P('stage', 'tp')
    chan_spec = P('stage', 'dp', None, None, 'tp')

    def device_step(act_in, w_conv, gamma_vec, beta_vec, z_grad):
        ci, co = w_conv.shape[3], w_conv.shape[4]
        w = w_conv[0].reshape(9, ci, co)
        vmem = pl.BlockSpec(memory_space=pltpu.VMEM)
        dma = pltpu.SemaphoreType.DMA
        z, dx, dw = pl.pallas_call(
            body,
            out_shape=(
                jax.ShapeDtypeStruct((8, SIDE, SIDE, co), BF16),
                jax.ShapeDtypeStruct((2, SIDE, SIDE, ci), BF16),
                jax.ShapeDtypeStruct((9, ci, co), F32),
            ),
            in_specs=[vmem, pl.BlockSpec(memory_space=pl.ANY), vmem, vmem, vmem],
            out_specs=[vmem, vmem, vmem],
            scratch_shapes=[
                pltpu.VMEM((LINE + 16 * PAIR, ci), BF16),
                pltpu.VMEM((9, ci, co), BF16),
                pltpu.VMEM((16, 2, IMG, co), BF16),
                pltpu.VMEM((3, LINE + 2 * PAIR + LINE, co), BF16),
                pltpu.VMEM((ci, 2 * PAIR), BF16),
                pltpu.VMEM((4, 2, IMG, ci), F32),
                pltpu.VMEM((4, ROWS, ci), F32),
                pltpu.VMEM((ROWS, ci), F32),
                pltpu.VMEM((2, ROWS, ci), BF16),
                pltpu.VMEM((ROWS, ci), BF16),
                pltpu.VMEM((8, ROWS, co), BF16),
                dma, dma((4, 4, 2)), dma((4, 2)), dma((2,)), dma((4, 2)), dma((2,)), dma((4, 2)), dma((4, 2)), dma((4, 2)), dma,
                dma((4, 4)), dma((4, 4)), dma((4,)), dma((4,)), dma, dma, dma, dma, dma((3,)), dma((3,)),
            ],
            compiler_params=pltpu.CompilerParams(collective_id=0, has_side_effects=True, vmem_limit_bytes=67043328),
            name='conv_block',
        )(act_in[0], w, gamma_vec, beta_vec, z_grad[0])
        return z[None], dx[None], dw.reshape(1, 3, 3, ci, co)

    return jax.shard_map(device_step, mesh=mesh, in_specs=(act_spec, w_spec, vec_spec, vec_spec, chan_spec), out_specs=(chan_spec, act_spec, w_spec), check_vma=False)
```

time: 430 us -> 144 us (0.33)
  waiting for transfers between devices: 241 us -> 0 us
  Pallas kernels: 0 us -> 125 us
  blocking collectives: 115 us -> 0 us
  matrix products: 40.2 us -> 0 us
  between operations: 14.8 us -> 0.64 us
  local copies, waits for them, and re-layouts: 5 us -> 18 us
  other arithmetic: 10.3 us -> 0 us
    psum x1 -> x0, waiting for transfers between devices: 174 us -> none  [device_step(): w_total = lax.psum(w_part, 'dp')]
    pallas_call x0 -> x1, Pallas kernels: none -> 125 us  [device_step(): pl.pallas_call(body, out_shape=(jax.ShapeDtypeStruct((8, SIDE, SIDE, co),...]
    unnamed x1 -> x0, blocking collectives: 115 us -> none
    conv_general_dilated x3 -> x0, matrix products: 40.2 us -> none  [the longest x1 15.3 us: conv_kernel_grad(): lax.conv_general_dilated(images, grad_map, (1, 1), ((1, 1), (1, 1)), dime...]
    ppermute x2 -> x0, waiting for transfers between devices: 35.5 us -> none  [the longest x1 20.2 us: device_step(): arrived = lax.ppermute(act_in[0], 'stage', perm=[(0, 1)])]
    all_gather x1 -> x0, waiting for transfers between devices: 31.6 us -> none  [device_step(): group_act = lax.all_gather(arrived, 'tp', axis=0, tiled=True)]
    unnamed x12 -> x5, local copies, waits for them, and re-layouts: 2.11 us -> 18 us
    broadcast_in_dim x2 -> x0, other arithmetic: 10.3 us -> none  [device_step(): return (z_keep[None], act_back[None], w_keep[None])]
  transfers between devices with their start and end apart: 4 -> 0, of which waited for: 4 -> 0; matrix products, arithmetic and copies ran while one was open for 4% -> 0% of each run, Pallas kernels for 0% -> 0%
where the time goes in v1:
time: 144 us; the launch traced here: 143 us
  Pallas kernels  125 us (87%)
  local copies, waits for them, and re-layouts  18 us (12%)
    pallas_call x1, Pallas kernels, device_step(): pl.pallas_call(body, out_shape=(jax.ShapeDtypeStruct((8, SIDE, SIDE, co),...  125 us
    unnamed x5, local copies, waits for them, and re-layouts  18 us

profile of v1, /device:TPU:6, one launch (start us, length us, event | category | flops | bytes accessed | tf_op | source)
XLA Modules:
  0.0 143.3 jit_solution(1683671568287059214)
XLA Ops:
  0.6 2.3 %copy.15 = bf16[1,2,14,14,1024]{4,3,2,1,0:T(8,128)(2,1)} copy(bf16[1,2,14,14,1024]{4,1,3,2,0:T(2,128)(2,1)} %param.5) | data formatting | bytes 1605632 | tf_op args[0]
  2.9 2.2 %copy.14 = bf16[1,8,14,14,256]{4,3,2,1,0:T(8,128)(2,1)} copy(bf16[1,8,14,14,256]{4,1,3,2,0:T(8,128)(2,1)} %param.9) | data formatting | bytes 1605632 | tf_op args[4]
  5.2 124.7 %conv_block.1 = (bf16[8,14,14,256]{3,2,1,0:T(8,128)(2,1)}, bf16[2,14,14,1024]{3,2,1,0:T(8,128)(2,1)}, f32[9,1024,256]{2,1,0:T(8,128)}) custom-call(bf16[2,14,14,1024]{3,2,1,0:T(8,128)(2,1)} %bitcast.12, bf16[9,1024,256]{2,1,0:T(8,128)(2,1)} %bitcast.11, f32[1,256]{1,0:T(1,128)} %gamma_ref.1, f32[1,256]{1,0:T(1,128)} %beta_ref.1, ...), custom_call_target="tpu_custom_call" | custom-call | tf_op jit(solution)/shard_map/conv_block/pallas_call | solution.py:398
  129.8 2.5 %copy.10 = bf16[1,8,14,14,256]{4,1,3,2,0:T(8,128)(2,1)} copy(bf16[1,8,14,14,256]{4,3,2,1,0:T(8,128)(2,1)} %bitcast.15) | data formatting | bytes 1605632
  132.3 2.9 %copy.11 = bf16[1,2,14,14,1024]{4,1,3,2,0:T(2,128)(2,1)} copy(bf16[1,2,14,14,1024]{4,3,2,1,0:T(8,128)(2,1)} %bitcast.14) | data formatting | bytes 1605632
  135.2 8.0 %copy.17 = f32[1,3,3,1024,256]{4,3,2,1,0:T(8,128)} copy(f32[1,3,3,1024,256]{4,3,2,1,0:T(8,128)} %bitcast.10) | data formatting | bytes 18874368

commit v2 on v1

--- a/solution.py
+++ b/solution.py
@@ -17,18 +17,53 @@
 IMG = 256
 PAIR = 2 * IMG
 NDP = 4
+M_PARTS = (pl.ds(0, 512), pl.ds(512, 512))
 GROUPS = ((0, 1), (2, 3), (4, 5), (6, 7), (8, 9), (12, 13), (10, 14), (11, 15))
 
 
-def widen(dst, n, src, m):
+def widen(dst, n, src):
     dst[n] = jnp.zeros(dst.shape[1:], BF16)
     for h in range(SIDE):
-        dst[n, pl.ds(h * LINE, SIDE), :] = src[m, h]
-
-
-def body(x_ref, w_hbm, gamma_ref, beta_ref, dz_ref, z_ref, dx_ref, dw_ref,
-         xbuf, wbuf, gbuf, gs, xt, dxp, dxd, dxx, xs, dxin, dzp,
-         w_sem, x_recv, y_send, yf_send, ring_send, x0_send, hop_send, near_send, far_send, early_send,
+        dst[n, pl.ds(h * LINE, SIDE), :] = src[h, :, n, :]
+
+
+def finish(x_hbm, g_hbm, part_hbm, out_hbm, xt, gs, acc, x_sem, g_sem, in_sem, out_sem):
+    x_copy = pltpu.make_async_copy(x_hbm, xt, x_sem)
+    g_copy = pltpu.make_async_copy(g_hbm, gs, g_sem)
+
+    def load(tap):
+        return pltpu.make_async_copy(part_hbm.at[tap], acc.at[tap], in_sem.at[tap])
+
+    def store(tap):
+        return pltpu.make_async_copy(acc.at[tap], out_hbm.at[tap], out_sem.at[tap])
+
+    x_copy.start()
+    g_copy.start()
+    for tap in range(3):
+        load(tap).start()
+    x_copy.wait()
+    g_copy.wait()
+    for tap in range(3, 9):
+        load(tap).start()
+
+    def step(dh, _):
+        for dw in range(3):
+            tap = dh * 3 + dw
+            rows = pl.ds(pl.multiple_of(2 * LINE - LINE * dh, LINE), 2 * PAIR)
+            load(tap).wait()
+            for at in M_PARTS:
+                acc[tap, at, :] += jnp.dot(xt[at, :], gs[dw, rows, :], preferred_element_type=F32)
+            store(tap).start()
+        return 0
+
+    lax.fori_loop(0, 3, step, 0)
+    for tap in range(9):
+        store(tap).wait()
+
+
+def body(x_ref, w_hbm, gamma_ref, beta_ref, dz_ref, z_ref, dx_ref, dw_hbm, xt, gs,
+         xbuf, wbuf, gbuf, dw_ref, dxp, dxd, dxx, xs, dxin, zf,
+         w_sem, dw_sem, x_recv, y_send, yf_send, ring_send, x0_send, hop_send, near_send, far_send, early_send,
          g_recv, g_send, d_recv, d_send, h_recv, h_send, b_recv, b_send, m_recv, m_send):
     dp = lax.axis_index('dp')
     stage = lax.axis_index('stage')
@@ -43,18 +78,22 @@
 
     w_copy = pltpu.make_async_copy(w_hbm, wbuf, w_sem)
 
+    def dw_copy(tap):
+        return pltpu.make_async_copy(dw_ref.at[tap], dw_hbm.at[tap], dw_sem.at[tap])
+
     @pl.when(stage == 1)
     def _():
         w_copy.start()
 
-    @pl.when(stage == 0)
-    def _():
-        for i in range(2):
-            widen(xs, i, x_ref, i)
-
     barrier = pltpu.get_barrier_semaphore()
     for peer in ((dp, 1 - stage, tp), (up, stage, tp), (down, stage, tp), (dp, stage, twin), (dp, stage, across)):
         pl.semaphore_signal(barrier, inc=1, device_id=peer, device_id_type=MESH)
+
+    @pl.when(stage == 0)
+    def _():
+        for i in range(2):
+            widen(xs, i, x_ref)
+
     pl.semaphore_wait(barrier, 5)
 
     def pair(k, j, i):
@@ -106,22 +145,25 @@
     own = pl.ds(0, ROWS)
 
     def h_copy():
-        return copy(dxp.at[2, 0, own, :], dxx, h_send, h_recv, (dp, 1, across))
+        return copy(dxp.at[3, 0, own, :], dxx, h_send, h_recv, (dp, 1, across))
 
     def b_copy():
         return copy(xs.at[0], dxin, b_send, b_recv, home)
 
     def m_far():
-        return copy(dxp.at[3, 0, own, :], dxd.at[0], m_send.at[0], m_recv.at[0], home)
+        return copy(dxp.at[2, 0, own, :], dxd.at[0], m_send.at[0], m_recv.at[0], home)
 
     def m_cross():
         return copy(dxd.at[0], dxd.at[1], m_send.at[1], m_recv.at[1], (dp, 0, across))
 
     def m_near():
-        return copy(dxp.at[1, 0, own, :], dxd.at[2], m_send.at[2], m_recv.at[2], home)
-
-    def narrow(value):
-        return value.reshape(SIDE, LINE, value.shape[-1])[:, :SIDE, :]
+        return copy(dxp.at[0, 0, own, :], dxd.at[2], m_send.at[2], m_recv.at[2], home)
+
+    def put_dx(i, value):
+        for h in range(SIDE):
+            dx_ref[h, :, i, :] = value[h * LINE:h * LINE + SIDE]
+
+    halves = [(b, pl.ds(b * 128, 128)) for b in range(co // 128)]
 
     @pl.when(stage == 0)
     def _():
@@ -129,7 +171,11 @@
             y_copy(0, i).start()
             ring_copy(1, i).start()
         dw_ref[...] = jnp.zeros_like(dw_ref)
+        for tap in range(9):
+            dw_copy(tap).start()
         z_ref[...] = jnp.zeros_like(z_ref)
+        xt[...] = jnp.zeros_like(xt)
+        gs[...] = jnp.zeros_like(gs)
         ring_copy(1, 0).wait_recv()
         ring_copy(2, 0).start()
         ring_copy(1, 1).wait_recv()
@@ -150,9 +196,9 @@
         m_cross().start()
         m_cross().wait_recv()
         m_near().wait_recv()
-        dx_ref[1] = narrow((dxd[2] + dxd[1]).astype(BF16))
+        put_dx(0, (dxd[2] + dxd[1]).astype(BF16))
         b_copy().wait_recv()
-        dx_ref[0] = narrow(dxin[...])
+        put_dx(1, dxin[...])
         for i in range(2):
             for k in range(4):
                 if (k, i) != (1, 0):
@@ -198,9 +244,12 @@
         for b in range(2):
             image = ((col + j - 2 * col * j) * 2 + (core + b - 2 * core * b)) * 2 + i
             part = affine[b * IMG:b * IMG + ROWS]
-            z_ref[image] = narrow(jnp.maximum(part, 0.0).astype(BF16))
-            dz = dzp[image].astype(F32)
-            gbuf[p, b, pl.ds(0, ROWS), :] = jnp.where(part > 0, dz * gamma_ref[...], 0.0).astype(BF16)
+            for c, lanes in halves:
+                aff = part[:, c * 128:c * 128 + 128]
+                at = pl.ds(image, ROWS, stride=8)
+                g = jnp.where(aff > 0, zf[c, at, :] * gamma_ref[:, lanes], 0.0)
+                gbuf[p, b, pl.ds(0, ROWS), lanes] = g.astype(BF16)
+                zf[c, at, :] = jnp.maximum(aff, 0.0)
         g_copy(1, p).start()
 
     def spread_g(p, at):
@@ -233,7 +282,7 @@
         d_copy(p).wait_recv()
         dxp[p, 0, own, :] += dxd[p]
 
-    def kernel_grad(first, second):
+    def prepare(first, second):
         spread_g(first, LINE)
         spread_g(second, LINE + PAIR)
 
@@ -247,10 +296,20 @@
 
         lax.fori_loop(0, 4, turn, 0)
 
+    def kernel_grad(first, second, last):
+        prepare(first, second)
+
         def step(dw, _):
             for dh in range(3):
                 rhs = gs[dw, pl.ds(LINE - LINE * (dh - 1), 2 * PAIR), :]
-                dw_ref[dh * 3 + dw] += jnp.dot(xt[...], rhs, preferred_element_type=F32)
+                for at in M_PARTS:
+                    dw_ref[dh * 3 + dw, at, :] += jnp.dot(xt[at, :], rhs, preferred_element_type=F32)
+
+            @pl.when(last)
+            def _():
+                for dh in range(3):
+                    dw_copy(dh * 3 + dw).start()
+
             return 0
 
         lax.fori_loop(0, 3, step, 0)
@@ -274,11 +333,10 @@
             for at in (0, LINE + PAIR, LINE + 2 * PAIR):
                 gs[dw, pl.ds(at, LINE), :] = jnp.zeros((LINE, co), BF16)
 
-        def widen_dz(n, _):
-            widen(dzp, n, dz_ref, n)
-            return 0
-
-        lax.fori_loop(0, 8, widen_dz, 0)
+        for h in range(SIDE):
+            for c, lanes in halves:
+                zf[c, pl.ds(h * 128, SIDE * 8), :] = dz_ref[h, :, :, lanes].astype(F32).reshape(SIDE * 8, 128)
+                zf[c, pl.ds(h * 128 + SIDE * 8, 16), :] = jnp.zeros((16, 128), F32)
         dw_ref[...] = jnp.zeros_like(dw_ref)
         dx_ref[...] = jnp.zeros_like(dx_ref)
         w_copy.wait()
@@ -289,83 +347,91 @@
         forward(0)
         input_grad(0)
         near(0, 1)
+        far(0, 0)
         near(1, 0)
-        far(0, 0)
+        dx_sum(0)
         near_copy(0, 1).wait_recv()
+        m_near().start()
         forward(1)
-        g_pass(1, 0)
         far_copy(0, 0).wait_recv()
         forward(2)
         input_grad(2)
+        g_pass(1, 0)
         far(0, 1)
         near(1, 1)
+        dx_sum(2)
+        g_pass(1, 1)
+        m_far().start()
+        input_grad(1)
         far_copy(0, 1).wait_recv()
         forward(3)
-        dx_sum(2)
-        g_pass(1, 1)
+        g_pass(1, 2)
+        input_grad(3)
+        near(2, 0)
+        far(1, 0)
+        dx_sum(1)
+        dx_sum(3)
+        g_pass(2, 0)
         h_copy().start()
-        input_grad(3)
-        g_pass(1, 2)
-        near(2, 0)
-        dx_sum(3)
-        far(1, 0)
-        m_far().start()
-        input_grad(1)
-        dx_sum(0)
-        g_pass(1, 3)
-        g_pass(2, 0)
-        dx_sum(1)
         g_pass(2, 1)
-        m_near().start()
+
+        for h in range(SIDE):
+            for c, lanes in halves:
+                z_ref[h, :, :, lanes] = zf[c, pl.ds(h * 128, SIDE * 8), :].reshape(SIDE, 8, 128).astype(BF16)
 
         def events(step):
             if step == 1:
                 near(2, 1)
                 far(1, 1)
+                g_pass(1, 3)
+            if step == 2:
                 g_pass(2, 2)
-                g_pass(2, 3)
-            if step == 2:
                 for i in range(2):
                     near_copy(1, i).wait_recv()
-                g_pass(3, 0)
             if step == 3:
                 near(3, 0)
                 for i in range(2):
                     far_copy(1, i).wait_recv()
-                g_pass(3, 1)
+                g_pass(3, 0)
             if step == 4:
                 near(3, 1)
                 for i in range(2):
                     near_copy(2, i).wait_recv()
-                g_pass(3, 2)
+                g_pass(2, 3)
+                g_pass(3, 1)
             if step == 5:
                 for i in range(2):
                     near_copy(3, i).wait_recv()
-                g_pass(3, 3)
+                g_pass(3, 2)
                 h_copy().wait_recv()
-                xs[0] = (dxp[0, 0, own, :] + dxx[...]).astype(BF16)
+                xs[0] = (dxp[1, 0, own, :] + dxx[...]).astype(BF16)
                 b_copy().start()
-            if step >= 6:
-                i = step - 6
-                far(2, i)
-                far(3, i)
-                far_copy(2, i).wait_recv()
-                far_copy(3, i).wait_recv()
+            if step == 6:
+                last_far(0)
+
+        def last_far(i):
+            far(2, i)
+            far(3, i)
+            far_copy(2, i).wait_recv()
+            far_copy(3, i).wait_recv()
 
         def run(step, _):
-            for s in range(1, 8):
+            for s in range(1, 7):
                 @pl.when(step == s)
                 def _(s=s):
                     events(s)
 
             first, second = (jnp.int32(v) for v in GROUPS[0])
-            for s in range(1, 8):
+            for s in range(1, 7):
                 first = jnp.where(step == s, GROUPS[s][0], first)
                 second = jnp.where(step == s, GROUPS[s][1], second)
-            kernel_grad(first, second)
+            kernel_grad(first, second, step == 6)
             return 0
 
-        lax.fori_loop(0, 8, run, 0)
+        lax.fori_loop(0, 7, run, 0)
+        last_far(1)
+        g_pass(3, 3)
+        prepare(*GROUPS[7])
 
         for i in range(2):
             for k in range(4):
@@ -383,6 +449,9 @@
         m_far().wait_send()
         m_near().wait_send()
 
+    for tap in range(9):
+        dw_copy(tap).wait()
+
 
 def solution(mesh):
     act_spec = P('stage', ('dp', 'tp'))
@@ -395,33 +464,50 @@
         w = w_conv[0].reshape(9, ci, co)
         vmem = pl.BlockSpec(memory_space=pltpu.VMEM)
         dma = pltpu.SemaphoreType.DMA
-        z, dx, dw = pl.pallas_call(
+        z, dx, dw, xt, gs = pl.pallas_call(
             body,
             out_shape=(
-                jax.ShapeDtypeStruct((8, SIDE, SIDE, co), BF16),
-                jax.ShapeDtypeStruct((2, SIDE, SIDE, ci), BF16),
+                jax.ShapeDtypeStruct((SIDE, SIDE, 8, co), BF16),
+                jax.ShapeDtypeStruct((SIDE, SIDE, 2, ci), BF16),
                 jax.ShapeDtypeStruct((9, ci, co), F32),
+                jax.ShapeDtypeStruct((ci, 2 * PAIR), BF16),
+                jax.ShapeDtypeStruct((3, LINE + 2 * PAIR + LINE, co), BF16),
             ),
             in_specs=[vmem, pl.BlockSpec(memory_space=pl.ANY), vmem, vmem, vmem],
-            out_specs=[vmem, vmem, vmem],
+            out_specs=[vmem, vmem, pl.BlockSpec(memory_space=pl.ANY), vmem, vmem],
             scratch_shapes=[
                 pltpu.VMEM((LINE + 16 * PAIR, ci), BF16),
                 pltpu.VMEM((9, ci, co), BF16),
                 pltpu.VMEM((16, 2, IMG, co), BF16),
-                pltpu.VMEM((3, LINE + 2 * PAIR + LINE, co), BF16),
-                pltpu.VMEM((ci, 2 * PAIR), BF16),
+                pltpu.VMEM((9, ci, co), F32),
                 pltpu.VMEM((4, 2, IMG, ci), F32),
                 pltpu.VMEM((4, ROWS, ci), F32),
                 pltpu.VMEM((ROWS, ci), F32),
                 pltpu.VMEM((2, ROWS, ci), BF16),
                 pltpu.VMEM((ROWS, ci), BF16),
-                pltpu.VMEM((8, ROWS, co), BF16),
-                dma, dma((4, 4, 2)), dma((4, 2)), dma((2,)), dma((4, 2)), dma((2,)), dma((4, 2)), dma((4, 2)), dma((4, 2)), dma,
+                pltpu.VMEM((co // 128, SIDE * 128, 128), F32),
+                dma, dma((9,)), dma((4, 4, 2)), dma((4, 2)), dma((2,)), dma((4, 2)), dma((2,)), dma((4, 2)), dma((4, 2)), dma((4, 2)), dma,
                 dma((4, 4)), dma((4, 4)), dma((4,)), dma((4,)), dma, dma, dma, dma, dma((3,)), dma((3,)),
             ],
             compiler_params=pltpu.CompilerParams(collective_id=0, has_side_effects=True, vmem_limit_bytes=67043328),
             name='conv_block',
-        )(act_in[0], w, gamma_vec, beta_vec, z_grad[0])
+        )(jnp.transpose(act_in[0], (1, 2, 0, 3)), w, gamma_vec, beta_vec, jnp.transpose(z_grad[0], (1, 2, 0, 3)))
+        hbm = pl.BlockSpec(memory_space=pl.ANY)
+        dw = pl.pallas_call(
+            finish,
+            out_shape=jax.ShapeDtypeStruct((9, ci, co), F32),
+            in_specs=[hbm, hbm, hbm],
+            out_specs=hbm,
+            scratch_shapes=[
+                pltpu.VMEM(xt.shape, BF16),
+                pltpu.VMEM(gs.shape, BF16),
+                pltpu.VMEM((9, ci, co), F32),
+                dma, dma, dma((9,)), dma((9,)),
+            ],
+            name='finish',
+        )(xt, gs, dw)
+        z = jnp.transpose(z, (2, 0, 1, 3))
+        dx = jnp.transpose(dx, (2, 0, 1, 3))
         return z[None], dx[None], dw.reshape(1, 3, 3, ci, co)
 
     return jax.shard_map(device_step, mesh=mesh, in_specs=(act_spec, w_spec, vec_spec, vec_spec, chan_spec), out_specs=(chan_spec, act_spec, w_spec), check_vma=False)

time: 144 us -> 124 us (0.86)
  local copies, waits for them, and re-layouts: 18 us -> 1.78 us
  Pallas kernels: 125 us -> 122 us
    unnamed x5 -> x6, local copies, waits for them, and re-layouts: 18 us -> 1.78 us
    pallas_call x1 -> x2, Pallas kernels: 125 us -> 122 us  [the longest x1 111 us: device_step(): pl.pallas_call(body, out_shape=(jax.ShapeDtypeStruct((SIDE, SIDE, 8, co),...]
where the time goes in v2:
time: 124 us
  Pallas kernels  122 us (98%)
  local copies, waits for them, and re-layouts  1.78 us (1%)
    pallas_call x1, Pallas kernels, device_step(): pl.pallas_call(body, out_shape=(jax.ShapeDtypeStruct((SIDE, SIDE, 8, co),...  111 us
    pallas_call x1, Pallas kernels, device_step(): pl.pallas_call(finish, out_shape=jax.ShapeDtypeStruct((9, ci, co), F32),...  10.4 us

profile of v2, /device:TPU:6, one launch (start us, length us, event | category | flops | bytes accessed | tf_op | source)
XLA Modules:
  0.0 124.1 jit_solution(1853506463270078664)
XLA Ops:
  0.6 111.3 %conv_block.1 = (bf16[14,14,8,256]{3,2,1,0:T(8,128)(2,1)}, bf16[14,14,2,1024]{3,2,1,0:T(2,128)(2,1)}, f32[9,1024,256]{2,1,0:T(8,128)}, bf16[1024,1024]{1,0:T(8,128)(2,1)}, bf16[3,1056,256]{2,1,0:T(8,128)(2,1)}) custom-call(bf16[14,14,2,1024]{3,2,1,0:T(2,128)(2,1)} %bitcast.18, bf16[9,1024,256]{2,1,0:T(8,128)(2,1)} %bitcast.15, f32[1,256]{1,0:T(1,128)} %gamma_ref.1, ...), custom_call_target="tpu_custom_call" | custom-call | tf_op jit(solution)/shard_map/conv_block/pallas_call | solution.py:467
  111.9 0.0 copy-start.1
  111.9 0.0 copy-start
  111.9 10.4 %finish.1 = f32[9,1024,256]{2,1,0:T(8,128)} custom-call(bf16[1024,1024]{1,0:T(8,128)(2,1)} %get-tuple-element.10.x_hbm, bf16[3,1056,256]{2,1,0:T(8,128)(2,1)} %get-tuple-element.11.g_hbm, f32[9,1024,256]{2,1,0:T(8,128)} %get-tuple-element.12.part_hbm), custom_call_target="tpu_custom_call" | custom-call | tf_op jit(solution)/shard_map/finish/pallas_call | solution.py:496
  122.3 0.0 copy-done.1
  122.3 0.9 copy.10
  123.2 0.0 copy-done
  123.2 0.9 copy.11
Async XLA Ops:
  111.9 10.4 %copy-start.1 = (bf16[14,14,8,256]{3,2,1,0:T(8,128)(2,1)S(1)}, bf16[14,14,8,256]{3,2,1,0:T(8,128)(2,1)}, u32[]{:S(2)}) copy-start(bf16[14,14,8,256]{3,2,1,0:T(8,128)(2,1)} %get-tuple-element.8) | copy-start | bytes 2408452
  111.9 11.3 %copy-start = (bf16[14,14,2,1024]{3,2,1,0:T(2,128)(2,1)S(1)}, bf16[14,14,2,1024]{3,2,1,0:T(2,128)(2,1)}, u32[]{:S(2)}) copy-start(bf16[14,14,2,1024]{3,2,1,0:T(2,128)(2,1)} %get-tuple-element.9) | copy-start | bytes 2408452

commit v3 on v2

--- a/solution.py
+++ b/solution.py
@@ -18,7 +18,7 @@
 PAIR = 2 * IMG
 NDP = 4
 M_PARTS = (pl.ds(0, 512), pl.ds(512, 512))
-GROUPS = ((0, 1), (2, 3), (4, 5), (6, 7), (8, 9), (12, 13), (10, 14), (11, 15))
+GROUPS = ((2, 3), (4, 5), (6, 7), (8, 9), (12, 13), (10, 14), (11, 15))
 
 
 def widen(dst, n, src):
@@ -286,6 +286,9 @@
         spread_g(first, LINE)
         spread_g(second, LINE + PAIR)
 
+        turn_in(0, 4, first, second)
+
+    def turn_in(begin, end, first, second):
         def turn(q, _):
             row = jnp.where(q < 2, first * 2 + q, second * 2 + q - 2)
             at = pl.ds(pl.multiple_of(LINE + row * IMG, LINE), IMG)
@@ -294,7 +297,7 @@
                 xt[pl.ds(c * 256, 256), to] = xbuf[at, pl.ds(c * 256, 256)].T
             return 0
 
-        lax.fori_loop(0, 4, turn, 0)
+        lax.fori_loop(begin, end, turn, 0)
 
     def kernel_grad(first, second, last):
         prepare(first, second)
@@ -341,11 +344,24 @@
         dx_ref[...] = jnp.zeros_like(dx_ref)
         w_copy.wait()
 
+        def early_grad(p):
+            turn_in(0, 2, p, p)
+
+            def step(dw, _):
+                for dh in range(3):
+                    rhs = gs[dw, pl.ds(LINE - LINE * (dh - 1), PAIR), :]
+                    for at in M_PARTS:
+                        dw_ref[dh * 3 + dw, at, :] += jnp.dot(xt[at, 0:PAIR], rhs, preferred_element_type=F32)
+                return 0
+
+            lax.fori_loop(0, 3, step, 0)
+
         near(0, 0)
         early_copy().start()
         near_copy(0, 0).wait_recv()
         forward(0)
         input_grad(0)
+        early_grad(0)
         near(0, 1)
         far(0, 0)
         near(1, 0)
@@ -363,6 +379,7 @@
         g_pass(1, 1)
         m_far().start()
         input_grad(1)
+        early_grad(1)
         far_copy(0, 1).wait_recv()
         forward(3)
         g_pass(1, 2)
@@ -379,34 +396,34 @@
             for c, lanes in halves:
                 z_ref[h, :, :, lanes] = zf[c, pl.ds(h * 128, SIDE * 8), :].reshape(SIDE, 8, 128).astype(BF16)
 
+        near(2, 1)
+        far(1, 1)
+
         def events(step):
             if step == 1:
-                near(2, 1)
-                far(1, 1)
                 g_pass(1, 3)
-            if step == 2:
                 g_pass(2, 2)
                 for i in range(2):
                     near_copy(1, i).wait_recv()
-            if step == 3:
+            if step == 2:
                 near(3, 0)
                 for i in range(2):
                     far_copy(1, i).wait_recv()
                 g_pass(3, 0)
-            if step == 4:
+            if step == 3:
                 near(3, 1)
                 for i in range(2):
                     near_copy(2, i).wait_recv()
                 g_pass(2, 3)
                 g_pass(3, 1)
-            if step == 5:
+            if step == 4:
                 for i in range(2):
                     near_copy(3, i).wait_recv()
                 g_pass(3, 2)
                 h_copy().wait_recv()
                 xs[0] = (dxp[1, 0, own, :] + dxx[...]).astype(BF16)
                 b_copy().start()
-            if step == 6:
+            if step == 5:
                 last_far(0)
 
         def last_far(i):
@@ -416,22 +433,22 @@
             far_copy(3, i).wait_recv()
 
         def run(step, _):
-            for s in range(1, 7):
+            for s in range(1, 6):
                 @pl.when(step == s)
                 def _(s=s):
                     events(s)
 
             first, second = (jnp.int32(v) for v in GROUPS[0])
-            for s in range(1, 7):
+            for s in range(1, 6):
                 first = jnp.where(step == s, GROUPS[s][0], first)
                 second = jnp.where(step == s, GROUPS[s][1], second)
-            kernel_grad(first, second, step == 6)
+            kernel_grad(first, second, step == 5)
             return 0
 
-        lax.fori_loop(0, 7, run, 0)
+        lax.fori_loop(0, 6, run, 0)
         last_far(1)
         g_pass(3, 3)
-        prepare(*GROUPS[7])
+        prepare(*GROUPS[6])
 
         for i in range(2):
             for k in range(4):

time: 124 us -> 122 us (0.984)
  Pallas kernels: 122 us -> 119 us
    pallas_call x1, Pallas kernels: 111 us -> 109 us  [device_step(): pl.pallas_call(body, out_shape=(jax.ShapeDtypeStruct((SIDE, SIDE, 8, co),...]
where the time goes in v3:
time: 122 us
  Pallas kernels  119 us (98%)
  local copies, waits for them, and re-layouts  1.78 us (1%)
    pallas_call x1, Pallas kernels, device_step(): pl.pallas_call(body, out_shape=(jax.ShapeDtypeStruct((SIDE, SIDE, 8, co),...  109 us
    pallas_call x1, Pallas kernels, device_step(): pl.pallas_call(finish, out_shape=jax.ShapeDtypeStruct((9, ci, co), F32),...  10.4 us

profile of v3, /device:TPU:6, one launch (start us, length us, event | category | flops | bytes accessed | tf_op | source)
XLA Modules:
  0.0 121.5 jit_solution(3536633223053946837)
XLA Ops:
  0.6 108.7 %conv_block.1 = (bf16[14,14,8,256]{3,2,1,0:T(8,128)(2,1)}, bf16[14,14,2,1024]{3,2,1,0:T(2,128)(2,1)}, f32[9,1024,256]{2,1,0:T(8,128)}, bf16[1024,1024]{1,0:T(8,128)(2,1)}, bf16[3,1056,256]{2,1,0:T(8,128)(2,1)}) custom-call(bf16[14,14,2,1024]{3,2,1,0:T(2,128)(2,1)} %bitcast.18, bf16[9,1024,256]{2,1,0:T(8,128)(2,1)} %bitcast.15, f32[1,256]{1,0:T(1,128)} %gamma_ref.1, ...), custom_call_target="tpu_custom_call" | custom-call | tf_op jit(solution)/shard_map/conv_block/pallas_call | solution.py:484
  109.4 0.0 copy-start.1
  109.4 0.0 copy-start
  109.4 10.4 %finish.1 = f32[9,1024,256]{2,1,0:T(8,128)} custom-call(bf16[1024,1024]{1,0:T(8,128)(2,1)} %get-tuple-element.10.x_hbm, bf16[3,1056,256]{2,1,0:T(8,128)(2,1)} %get-tuple-element.11.g_hbm, f32[9,1024,256]{2,1,0:T(8,128)} %get-tuple-element.12.part_hbm), custom_call_target="tpu_custom_call" | custom-call | tf_op jit(solution)/shard_map/finish/pallas_call | solution.py:513
  119.8 0.0 copy-done.1
  119.8 0.9 copy.10
  120.7 0.0 copy-done
  120.7 0.9 copy.11
Async XLA Ops:
  109.4 10.4 %copy-start.1 = (bf16[14,14,8,256]{3,2,1,0:T(8,128)(2,1)S(1)}, bf16[14,14,8,256]{3,2,1,0:T(8,128)(2,1)}, u32[]{:S(2)}) copy-start(bf16[14,14,8,256]{3,2,1,0:T(8,128)(2,1)} %get-tuple-element.8) | copy-start | bytes 2408452
  109.4 11.3 %copy-start = (bf16[14,14,2,1024]{3,2,1,0:T(2,128)(2,1)S(1)}, bf16[14,14,2,1024]{3,2,1,0:T(2,128)(2,1)}, u32[]{:S(2)}) copy-start(bf16[14,14,2,1024]{3,2,1,0:T(2,128)(2,1)} %get-tuple-element.9) | copy-start | bytes 2408452

commit v4 on v3

--- a/solution.py
+++ b/solution.py
@@ -414,16 +414,16 @@
                 near(3, 1)
                 for i in range(2):
                     near_copy(2, i).wait_recv()
-                g_pass(2, 3)
-                g_pass(3, 1)
             if step == 4:
                 for i in range(2):
                     near_copy(3, i).wait_recv()
-                g_pass(3, 2)
+                g_pass(2, 3)
+                g_pass(3, 1)
                 h_copy().wait_recv()
                 xs[0] = (dxp[1, 0, own, :] + dxx[...]).astype(BF16)
                 b_copy().start()
             if step == 5:
+                g_pass(3, 2)
                 last_far(0)
 
         def last_far(i):

time: 122 us -> 121 us (level)
  no operation moved by 1% of the time
where the time goes in v4:
time: 121 us
  Pallas kernels  118 us (98%)
  local copies, waits for them, and re-layouts  1.78 us (1%)
    pallas_call x1, Pallas kernels, device_step(): pl.pallas_call(body, out_shape=(jax.ShapeDtypeStruct((SIDE, SIDE, 8, co),...  108 us
    pallas_call x1, Pallas kernels, device_step(): pl.pallas_call(finish, out_shape=jax.ShapeDtypeStruct((9, ci, co), F32),...  10.4 us

profile of v4, /device:TPU:6, one launch (start us, length us, event | category | flops | bytes accessed | tf_op | source)
XLA Modules:
  0.0 120.8 jit_solution(12944187314394395194)
XLA Ops:
  0.6 107.9 %conv_block.1 = (bf16[14,14,8,256]{3,2,1,0:T(8,128)(2,1)}, bf16[14,14,2,1024]{3,2,1,0:T(2,128)(2,1)}, f32[9,1024,256]{2,1,0:T(8,128)}, bf16[1024,1024]{1,0:T(8,128)(2,1)}, bf16[3,1056,256]{2,1,0:T(8,128)(2,1)}) custom-call(bf16[14,14,2,1024]{3,2,1,0:T(2,128)(2,1)} %bitcast.18, bf16[9,1024,256]{2,1,0:T(8,128)(2,1)} %bitcast.15, f32[1,256]{1,0:T(1,128)} %gamma_ref.1, ...), custom_call_target="tpu_custom_call" | custom-call | tf_op jit(solution)/shard_map/conv_block/pallas_call | solution.py:484
  108.6 0.0 copy-start.1
  108.6 0.0 copy-start
  108.6 10.4 %finish.1 = f32[9,1024,256]{2,1,0:T(8,128)} custom-call(bf16[1024,1024]{1,0:T(8,128)(2,1)} %get-tuple-element.10.x_hbm, bf16[3,1056,256]{2,1,0:T(8,128)(2,1)} %get-tuple-element.11.g_hbm, f32[9,1024,256]{2,1,0:T(8,128)} %get-tuple-element.12.part_hbm), custom_call_target="tpu_custom_call" | custom-call | tf_op jit(solution)/shard_map/finish/pallas_call | solution.py:513
  119.0 0.0 copy-done.1
  119.0 0.9 copy.10
  119.9 0.0 copy-done
  119.9 0.9 copy.11
Async XLA Ops:
  108.6 10.4 %copy-start.1 = (bf16[14,14,8,256]{3,2,1,0:T(8,128)(2,1)S(1)}, bf16[14,14,8,256]{3,2,1,0:T(8,128)(2,1)}, u32[]{:S(2)}) copy-start(bf16[14,14,8,256]{3,2,1,0:T(8,128)(2,1)} %get-tuple-element.8) | copy-start | bytes 2408452
  108.6 11.3 %copy-start = (bf16[14,14,2,1024]{3,2,1,0:T(2,128)(2,1)S(1)}, bf16[14,14,2,1024]{3,2,1,0:T(2,128)(2,1)}, u32[]{:S(2)}) copy-start(bf16[14,14,2,1024]{3,2,1,0:T(2,128)(2,1)} %get-tuple-element.9) | copy-start | bytes 2408452
